TPU v7x, 32 devices: a whole 2x2x4 slice. The times are simulated.
32 devices in a mesh: gx: 2 (over y), gy: 4 (over x, core), gz: 4 (over z).
Axes of the slice: x: 2, y: 2, z: 4, core: 2. Of those that a mesh axis runs over, the one named last changes fastest.
Arguments:
- volume: float32 [16, 64, 512], P(('gx', 'gy'), None, 'gz'), may hold values from 0 to 1
- levels: int32 [4], replicated, may hold values from 0 to 255
Outputs:
- labelling: float32 [4, 16, 64, 512], P(None, 'gx', 'gy', 'gz')
- centers: float32 [4], replicated
All inputs are finite; a program needn't handle non-finite values.
Results may differ from a plain program's by a relative error of at most 0.0001.
Values sent between devices are 32-bit elements; how exact they have to be, the bound alone decides.
A program may use at most 64 MiB of HBM per device.

v0:
```python
import jax
import jax.numpy as jnp
from jax import lax
from jax.sharding import PartitionSpec as P

ITERS = 2
tau_step = 0.25
sigma_step = 0.25
smooth_weight = 0.5
prior_weight = 1.0


def with_halo(block, sides, width):
    for axis, dim in sides:
        count = lax.axis_size(axis)
        forward = [(i, i + 1) for i in range(count - 1)]
        backward = [(target, source) for source, target in forward]
        low = lax.ppermute(
            lax.slice_in_dim(block, block.shape[dim] - width, None, axis=dim), axis, forward
        )
        high = lax.ppermute(lax.slice_in_dim(block, 0, width, axis=dim), axis, backward)
        block = jnp.concatenate([low, block, high], axis=dim)
    return block


def project_simplex(values):
    how_many = values.shape[0]
    threshold = None
    for subset in range(1, 1 << how_many):
        members = [label_index for label_index in range(how_many) if subset >> label_index & 1]
        summed = values[members[0]]
        for label_index in members[1:]:
            summed = summed + values[label_index]
        candidate = (summed - 1.0) / float(len(members))
        threshold = candidate if threshold is None else jnp.maximum(threshold, candidate)
    return jnp.maximum(values - threshold[None], 0.0)


def bounds(start, total, extent):
    position = start - 1 + jnp.arange(extent + 1, dtype=jnp.int32)
    return (position >= 0, position < total - 1)


def local(volume, levels):
    thickness = volume.shape[0]
    x_start = (lax.axis_index("gx") * lax.axis_size("gy") + lax.axis_index("gy")) * thickness
    x_total = thickness * lax.axis_size("gx") * lax.axis_size("gy")
    y_start = 0
    y_total = volume.shape[1]
    z_start = lax.axis_index("gz") * volume.shape[2]
    z_total = volume.shape[2] * lax.axis_size("gz")
    extent = volume.shape
    how_many = levels.shape[0]
    inside_x, ahead_x = bounds(x_start, x_total, extent[0])
    inside_y, ahead_y = bounds(y_start, y_total, extent[1])
    inside_z, ahead_z = bounds(z_start, z_total, extent[2])
    inside = (inside_x[:, None, None] & inside_y[None, :, None] & inside_z[None, None, :]).astype(
        jnp.float32
    )
    base_levels = levels.astype(jnp.float32) / 255.0
    centers = base_levels
    starting = (volume[None] - base_levels[:, None, None, None]) ** 2
    labelling = project_simplex(1.0 / how_many - tau_step * starting)
    smoothed = labelling
    dual_field = jnp.zeros((how_many, 3, extent[0] + 1, extent[1] + 1, extent[2] + 1), jnp.float32)
    for iteration in range(ITERS):
        padded = with_halo(smoothed, ((("gx", "gy"), 1), ("gz", 3)), 1)
        padded = jnp.pad(padded, ((0, 0), (0, 0), (1, 1), (0, 0)))
        corner = padded[:, :-1, :-1, :-1]
        grad_x = jnp.where(ahead_x[:, None, None], padded[:, 1:, :-1, :-1] - corner, 0.0)
        grad_y = jnp.where(ahead_y[None, :, None], padded[:, :-1, 1:, :-1] - corner, 0.0)
        grad_z = jnp.where(ahead_z[None, None, :], padded[:, :-1, :-1, 1:] - corner, 0.0)
        stepped = dual_field + sigma_step * jnp.stack([grad_x, grad_y, grad_z], axis=1)
        length = jnp.sqrt(
            stepped[:, 0] * stepped[:, 0]
            + stepped[:, 1] * stepped[:, 1]
            + stepped[:, 2] * stepped[:, 2]
        )
        shrink = inside / jnp.maximum(1.0, length / smooth_weight)
        dual_field = stepped * shrink[:, None]
        divergence = (
            dual_field[:, 0, 1:, 1:, 1:]
            - dual_field[:, 0, :-1, 1:, 1:]
            + (dual_field[:, 1, 1:, 1:, 1:] - dual_field[:, 1, 1:, :-1, 1:])
            + (dual_field[:, 2, 1:, 1:, 1:] - dual_field[:, 2, 1:, 1:, :-1])
        )
        fidelity = (volume[None] - centers[:, None, None, None]) ** 2
        updated = project_simplex(labelling + tau_step * (divergence - fidelity))
        smoothed = 2.0 * updated - labelling
        labelling = updated
        sizes_local = jnp.sum(labelling, axis=(1, 2, 3))
        weighted = jnp.sum(labelling * volume[None], axis=(1, 2, 3))
        sizes_all, weighted_all = lax.psum((sizes_local, weighted), ("gx", "gy", "gz"))
        centers = (weighted_all + prior_weight * base_levels) / (sizes_all + prior_weight)
    labelling = lax.all_to_all(labelling, "gy", split_axis=2, concat_axis=1, tiled=True)
    return (labelling, centers)


def solution(mesh):
    return jax.shard_map(
        local,
        mesh=mesh,
        in_specs=(P(("gx", "gy"), None, "gz"), P()),
        out_specs=(P(None, "gx", "gy", "gz"), P()),
        check_vma=False,
    )
```

profile of v0, /device:TPU:0, one launch (start us, length us, event | category | flops | bytes accessed | tf_op | source)
XLA Modules:
  0.0 159.2 jit_solution(3588290688517704985)
XLA Ops:
  1.3 0.9 multiply_subtract_fusion.1
  3.0 1.0 subtract_maximum_fusion.2
  4.0 2.4 %collective-permute-start = (f32[4,1,64,128]{3,2,1,0:T(8,128)S(1)}, f32[4,1,64,128]{3,2,1,0:T(8,128)S(1)}, u32[]{:S(2)}, u32[]{:S(2)}) collective-permute-start(f32[4,1,64,128]{3,2,1,0:T(8,128)S(1)} %get-tuple-element.24), channel_id=1, source_target_pairs={{0,4},{4,8},{8,12},{12,16},{16,20},{20,24},{24,28},{1,5},{5,9},{9,... | collective-permute-start | bytes 393224 | tf_op jit(solution)/shard_map/ppermute | solution.py:18
  6.4 1.3 collective-permute-start.1
  8.0 3.7 %collective-permute-done.1 = f32[4,1,64,128]{3,2,1,0:T(8,128)S(1)} collective-permute-done((f32[4,1,64,128]{3,2,1,0:T(8,128)S(1)}, f32[4,1,64,128]{3,2,1,0:T(8,128)S(1)}, u32[]{:S(2)}, u32[]{:S(2)}) %collective-permute-start.1) | collective-permute-done | bytes 131104 | tf_op jit(solution)/shard_map/ppermute | solution.py:21
  12.0 3.5 %collective-permute-start.2 = (f32[4,4,64,1]{3,2,1,0:T(8,128)S(1)}, f32[4,4,64,1]{3,2,1,0:T(8,128)S(1)}, u32[]{:S(2)}, u32[]{:S(2)}) collective-permute-start(f32[4,4,64,1]{3,2,1,0:T(8,128)S(1)} %get-tuple-element.19), channel_id=1, source_target_pairs={{0,1},{1,2},{2,3},{4,5},{5,6},{6,7},{8,9},{9,10},{10,11},{12,13},{... | collective-permute-start | bytes 12296 | tf_op jit(solution)/shard_map/ppermute | solution.py:18
  15.5 1.3 collective-permute-start.3
  16.8 8.4 %collective-permute-done.2 = f32[4,4,64,1]{3,2,1,0:T(8,128)S(1)} collective-permute-done((f32[4,4,64,1]{3,2,1,0:T(8,128)S(1)}, f32[4,4,64,1]{3,2,1,0:T(8,128)S(1)}, u32[]{:S(2)}, u32[]{:S(2)}) %collective-permute-start.2) | collective-permute-done | bytes 4128 | tf_op jit(solution)/shard_map/ppermute | solution.py:18
  25.2 4.7 %collective-permute-done.3 = f32[4,4,64,1]{3,2,1,0:T(8,128)S(1)} collective-permute-done((f32[4,4,64,1]{3,2,1,0:T(8,128)S(1)}, f32[4,4,64,1]{3,2,1,0:T(8,128)S(1)}, u32[]{:S(2)}, u32[]{:S(2)}) %collective-permute-start.3) | collective-permute-done | bytes 4128 | tf_op jit(solution)/shard_map/ppermute | solution.py:21
  33.1 0.9 copy-done
  34.1 1.1 multiply_reduce_fusion.1
  36.6 4.7 %collective-permute-start.4 = (f32[4,1,64,128]{3,2,1,0:T(8,128)}, f32[4,1,64,128]{3,2,1,0:T(8,128)}, u32[]{:S(2)}, u32[]{:S(2)}) collective-permute-start(f32[4,1,64,128]{3,2,1,0:T(8,128)} %get-tuple-element.22), channel_id=1, source_target_pairs={{0,4},{4,8},{8,12},{12,16},{16,20},{20,24},{24,28},{1,5},{5,9},{9,... | collective-permute-start | bytes 393224 | tf_op jit(solution)/shard_map/ppermute | solution.py:18
  41.3 1.3 collective-permute-start.5
  42.6 44.4 %all-reduce.3 = (f32[4]{0:T(128)}, f32[4]{0:T(128)}) all-reduce(f32[4]{0:T(128)} %get-tuple-element.3, f32[4]{0:T(128)} %get-tuple-element.2), channel_id=1, replica_groups=mesh['gx'=2,'gy'=4,'gz'=4] {'gx','gy','gz'}, use_global_device_ids=true, to_apply=%region_3.4 | all-reduce | flops 8 | bytes 64 | tf_op jit(solution)/shard_map/psum | solution.py:93
  87.0 1.1 pad_maximum_fusion.2
  88.4 2.3 %collective-permute-start.6 = (f32[4,4,64,1]{3,2,1,0:T(8,128)S(1)}, f32[4,4,64,1]{3,2,1,0:T(8,128)S(1)}, u32[]{:S(2)}, u32[]{:S(2)}) collective-permute-start(f32[4,4,64,1]{3,2,1,0:T(8,128)S(1)} %get-tuple-element.17), channel_id=1, source_target_pairs={{0,1},{1,2},{2,3},{4,5},{5,6},{6,7},{8,9},{9,10},{10,11},{12,13},{... | collective-permute-start | bytes 12296 | tf_op jit(solution)/shard_map/ppermute | solution.py:18
  90.7 1.3 collective-permute-start.7
  92.1 9.2 %collective-permute-done.6 = f32[4,4,64,1]{3,2,1,0:T(8,128)S(1)} collective-permute-done((f32[4,4,64,1]{3,2,1,0:T(8,128)S(1)}, f32[4,4,64,1]{3,2,1,0:T(8,128)S(1)}, u32[]{:S(2)}, u32[]{:S(2)}) %collective-permute-start.6) | collective-permute-done | bytes 4128 | tf_op jit(solution)/shard_map/ppermute | solution.py:18
  101.3 4.1 %collective-permute-done.7 = f32[4,4,64,1]{3,2,1,0:T(8,128)S(1)} collective-permute-done((f32[4,4,64,1]{3,2,1,0:T(8,128)S(1)}, f32[4,4,64,1]{3,2,1,0:T(8,128)S(1)}, u32[]{:S(2)}, u32[]{:S(2)}) %collective-permute-start.7) | collective-permute-done | bytes 4128 | tf_op jit(solution)/shard_map/ppermute | solution.py:21
  105.5 1.5 select_maximum_fusion
  109.4 1.2 copy-done.1
  111.6 0.9 copy.8
  112.5 3.9 %all-to-all-start = ((f32[4,2,64,128]{3,1,0,2:T(2,128)}), f32[4,2,64,128]{3,1,0,2:T(2,128)S(1)}, u32[]{:S(2)}, u32[]{:S(2)}) async-start(f32[4,2,64,128]{3,1,0,2:T(2,128)} %copy.8), calls=%async_computation | async-start | bytes 524288 | tf_op jit(solution)/shard_map/all_to_all | solution.py:95
  116.4 41.5 %all-reduce.2 = (f32[4]{0:T(128)S(1)}, f32[4]{0:T(128)S(1)}) all-reduce(f32[4]{0:T(128)S(1)} %get-tuple-element.5, f32[4]{0:T(128)S(1)} %get-tuple-element.4), channel_id=1, replica_groups=mesh['gx'=2,'gy'=4,'gz'=4] {'gx','gy','gz'}, use_global_device_ids=true, to_apply=%region_7.8 | all-reduce | flops 8 | bytes 64 | tf_op jit(solution)/shard_map/psum | solution.py:93
  (71 shorter events, 11.4 us)
Async XLA Ops:
  4.0 4.0 %collective-permute-start = (f32[4,1,64,128]{3,2,1,0:T(8,128)S(1)}, f32[4,1,64,128]{3,2,1,0:T(8,128)S(1)}, u32[]{:S(2)}, u32[]{:S(2)}) collective-permute-start(f32[4,1,64,128]{3,2,1,0:T(8,128)S(1)} %get-tuple-element.24), channel_id=1, source_target_pairs={{0,4},{4,8},{8,12},{12,16},{16,20},{20,24},{24,28},{1,5},{5,9},{9,... | collective-permute-start | bytes 393224 | tf_op jit(solution)/shard_map/ppermute | solution.py:18
  6.4 5.3 %collective-permute-start.1 = (f32[4,1,64,128]{3,2,1,0:T(8,128)S(1)}, f32[4,1,64,128]{3,2,1,0:T(8,128)S(1)}, u32[]{:S(2)}, u32[]{:S(2)}) collective-permute-start(f32[4,1,64,128]{3,2,1,0:T(8,128)S(1)} %get-tuple-element.25), channel_id=1, source_target_pairs={{4,0},{8,4},{12,8},{16,12},{20,16},{24,20},{28,24},{5,1},{9,5},{13... | collective-permute-start | bytes 393224 | tf_op jit(solution)/shard_map/ppermute | solution.py:21
  7.9 23.2 %copy-start.6 = (f32[3,65,129]{2,1,0:T(8,128)}, f32[3,65,129]{2,1,0:T(8,128)S(1)}, u32[]{:S(2)}) copy-start(f32[3,65,129]{2,1,0:T(8,128)S(1)} %and_convert_fusion) | copy-start | bytes 301864
  12.0 13.2 %collective-permute-start.2 = (f32[4,4,64,1]{3,2,1,0:T(8,128)S(1)}, f32[4,4,64,1]{3,2,1,0:T(8,128)S(1)}, u32[]{:S(2)}, u32[]{:S(2)}) collective-permute-start(f32[4,4,64,1]{3,2,1,0:T(8,128)S(1)} %get-tuple-element.19), channel_id=1, source_target_pairs={{0,1},{1,2},{2,3},{4,5},{5,6},{6,7},{8,9},{9,10},{10,11},{12,13},{... | collective-permute-start | bytes 12296 | tf_op jit(solution)/shard_map/ppermute | solution.py:18
  15.5 14.4 %collective-permute-start.3 = (f32[4,4,64,1]{3,2,1,0:T(8,128)S(1)}, f32[4,4,64,1]{3,2,1,0:T(8,128)S(1)}, u32[]{:S(2)}, u32[]{:S(2)}) collective-permute-start(f32[4,4,64,1]{3,2,1,0:T(8,128)S(1)} %get-tuple-element.20), channel_id=1, source_target_pairs={{1,0},{2,1},{3,2},{5,4},{6,5},{7,6},{9,8},{10,9},{11,10},{13,12},{... | collective-permute-start | bytes 12296 | tf_op jit(solution)/shard_map/ppermute | solution.py:21
  16.8 14.1 %copy-start.14 = (pred[65]{0:T(512)(128)(4,1)}, pred[65]{0:T(512)(128)(4,1)S(1)}, u32[]{:S(2)}) copy-start(pred[65]{0:T(512)(128)(4,1)S(1)} %fusion.62) | copy-start | bytes 199
  31.7 0.9 copy-start.9
  32.5 1.5 copy-start
  34.1 2.6 %copy-start.11 = (f32[2,64,128]{2,1,0:T(8,128)}, f32[2,64,128]{2,1,0:T(8,128)S(1)}, u32[]{:S(2)}) copy-start(f32[2,64,128]{2,1,0:T(8,128)S(1)} %maximum_bitcast_fusion.1) | copy-start | bytes 196612
  34.1 58.0 %copy-start.13 = (s32[4]{0:T(128)S(1)}, s32[4]{0:T(128)}, u32[]{:S(2)}) copy-start(s32[4]{0:T(128)} %param.3) | copy-start | bytes 52
  36.6 50.4 %collective-permute-start.4 = (f32[4,1,64,128]{3,2,1,0:T(8,128)}, f32[4,1,64,128]{3,2,1,0:T(8,128)}, u32[]{:S(2)}, u32[]{:S(2)}) collective-permute-start(f32[4,1,64,128]{3,2,1,0:T(8,128)} %get-tuple-element.22), channel_id=1, source_target_pairs={{0,4},{4,8},{8,12},{12,16},{16,20},{20,24},{24,28},{1,5},{5,9},{9,... | collective-permute-start | bytes 393224 | tf_op jit(solution)/shard_map/ppermute | solution.py:18
  41.3 45.7 %collective-permute-start.5 = (f32[4,1,64,128]{3,2,1,0:T(8,128)}, f32[4,1,64,128]{3,2,1,0:T(8,128)}, u32[]{:S(2)}, u32[]{:S(2)}) collective-permute-start(f32[4,1,64,128]{3,2,1,0:T(8,128)} %get-tuple-element.23), channel_id=1, source_target_pairs={{4,0},{8,4},{12,8},{16,12},{20,16},{24,20},{28,24},{5,1},{9,5},{13... | collective-permute-start | bytes 393224 | tf_op jit(solution)/shard_map/ppermute | solution.py:21
  87.0 5.0 %copy-start.16 = (f32[4]{0:T(128)S(1)}, f32[4]{0:T(128)}, u32[]{:S(2)}) copy-start(f32[4]{0:T(128)} %get-tuple-element.8) | copy-start | bytes 52
  87.0 5.0 %copy-start.17 = (f32[4]{0:T(128)S(1)}, f32[4]{0:T(128)}, u32[]{:S(2)}) copy-start(f32[4]{0:T(128)} %get-tuple-element.9) | copy-start | bytes 52
  87.0 18.4 %copy-start.3 = (f32[4,2,64,128]{3,2,1,0:T(8,128)S(1)}, f32[4,2,64,128]{3,2,1,0:T(8,128)}, u32[]{:S(2)}) copy-start(f32[4,2,64,128]{3,2,1,0:T(8,128)} %copy-done.2) | copy-start | bytes 786436
  88.2 18.8 %copy-start.15 = (pred[65]{0:T(512)(128)(4,1)S(1)}, pred[65]{0:T(512)(128)(4,1)}, u32[]{:S(2)}) copy-start(pred[65]{0:T(512)(128)(4,1)} %copy-done.14) | copy-start | bytes 199
  88.4 12.9 %collective-permute-start.6 = (f32[4,4,64,1]{3,2,1,0:T(8,128)S(1)}, f32[4,4,64,1]{3,2,1,0:T(8,128)S(1)}, u32[]{:S(2)}, u32[]{:S(2)}) collective-permute-start(f32[4,4,64,1]{3,2,1,0:T(8,128)S(1)} %get-tuple-element.17), channel_id=1, source_target_pairs={{0,1},{1,2},{2,3},{4,5},{5,6},{6,7},{8,9},{9,10},{10,11},{12,13},{... | collective-permute-start | bytes 12296 | tf_op jit(solution)/shard_map/ppermute | solution.py:18
  90.7 14.7 %collective-permute-start.7 = (f32[4,4,64,1]{3,2,1,0:T(8,128)S(1)}, f32[4,4,64,1]{3,2,1,0:T(8,128)S(1)}, u32[]{:S(2)}, u32[]{:S(2)}) collective-permute-start(f32[4,4,64,1]{3,2,1,0:T(8,128)S(1)} %get-tuple-element.18), channel_id=1, source_target_pairs={{1,0},{2,1},{3,2},{5,4},{6,5},{7,6},{9,8},{10,9},{11,10},{13,12},{... | collective-permute-start | bytes 12296 | tf_op jit(solution)/shard_map/ppermute | solution.py:21
  107.4 0.9 copy-start.7
  108.8 1.8 %copy-start.1 = (f32[4,3,3,65,129]{4,3,2,0,1:T(8,128)S(1)}, f32[4,3,3,65,129]{4,3,2,0,1:T(8,128)}, u32[]{:S(2)}) copy-start(f32[4,3,3,65,129]{4,3,2,0,1:T(8,128)} %copy-done) | copy-start | bytes 3622324
  108.8 1.7 %copy-start.5 = (f32[2,64,128]{2,1,0:T(8,128)S(1)}, f32[2,64,128]{2,1,0:T(8,128)}, u32[]{:S(2)}) copy-start(f32[2,64,128]{2,1,0:T(8,128)} %param.2) | copy-start | bytes 196612
  108.8 1.7 %copy-start.10 = (f32[2,64,128]{2,1,0:T(8,128)S(1)}, f32[2,64,128]{2,1,0:T(8,128)}, u32[]{:S(2)}) copy-start(f32[2,64,128]{2,1,0:T(8,128)} %copy-done.8) | copy-start | bytes 196612
  108.8 1.7 %copy-start.12 = (f32[2,64,128]{2,1,0:T(8,128)S(1)}, f32[2,64,128]{2,1,0:T(8,128)}, u32[]{:S(2)}) copy-start(f32[2,64,128]{2,1,0:T(8,128)} %copy-done.11) | copy-start | bytes 196612
  112.5 45.9 %all-to-all-start = ((f32[4,2,64,128]{3,1,0,2:T(2,128)}), f32[4,2,64,128]{3,1,0,2:T(2,128)S(1)}, u32[]{:S(2)}, u32[]{:S(2)}) async-start(f32[4,2,64,128]{3,1,0,2:T(2,128)} %copy.8), calls=%async_computation | async-start | bytes 524288 | tf_op jit(solution)/shard_map/all_to_all | solution.py:95
  (3 other events, 2.2 us)
where the time goes:
time: 160 us; the launch traced here: 159 us
  blocking collectives  85.9 us (54%)
  waiting for transfers between devices  30.2 us (19%)
  starting transfers between devices  22 us (14%)
  other arithmetic  12.8 us (8%)
  local copies, waits for them, and re-layouts  7.36 us (5%)
    psum x2, blocking collectives, local(): lax.psum((sizes_local, weighted), ('gx', 'gy', 'gz'))  85.9 us
    ppermute x4, waiting for transfers between devices, with_halo(): lax.ppermute(lax.slice_in_dim(block, block.shape[dim] - width, None, axis...  17.6 us
    ppermute x4, starting transfers between devices, with_halo(): lax.ppermute(lax.slice_in_dim(block, block.shape[dim] - width, None, axis...  12.9 us
    ppermute x4, waiting for transfers between devices, with_halo(): lax.ppermute(lax.slice_in_dim(block, 0, width, axis=dim), axis, backward)  12.6 us
    ppermute x4, starting transfers between devices, with_halo(): lax.ppermute(lax.slice_in_dim(block, 0, width, axis=dim), axis, backward)  5.16 us
    unnamed x36, local copies, waits for them, and re-layouts  4.51 us
    all_to_all x1, starting transfers between devices, local(): lax.all_to_all(labelling, 'gy', split_axis=2, concat_axis=1, tiled=True)  3.9 us
  transfers between devices with their start and end apart: 9, of which 5 were waited for; matrix products, arithmetic and copies ran while one was open for 0% of the time, Pallas kernels for 0%

commit v1 on v0

--- a/solution.py
+++ b/solution.py
@@ -90,7 +90,7 @@
         labelling = updated
         sizes_local = jnp.sum(labelling, axis=(1, 2, 3))
         weighted = jnp.sum(labelling * volume[None], axis=(1, 2, 3))
-        sizes_all, weighted_all = lax.psum((sizes_local, weighted), ("gx", "gy", "gz"))
+        sizes_all, weighted_all = lax.psum(lax.psum((sizes_local, weighted), "gx"), ("gy", "gz"))
         centers = (weighted_all + prior_weight * base_levels) / (sizes_all + prior_weight)
     labelling = lax.all_to_all(labelling, "gy", split_axis=2, concat_axis=1, tiled=True)
     return (labelling, centers)

time: 160 us -> 149 us (0.931)
  blocking collectives: 85.9 us -> 77.6 us
  waiting for transfers between devices: 30.2 us -> 27.4 us
    psum x2 -> x4, blocking collectives: 85.9 us -> 77.6 us  [the longest x2 62.5 us: local(): lax.psum(lax.psum((sizes_local, weighted), 'gx'), ('gy', 'gz'))]
    ppermute x4, waiting for transfers between devices: 17.6 us -> 14.8 us  [with_halo(): lax.ppermute(lax.slice_in_dim(block, block.shape[dim] - width, None, axis...]
  transfers between devices with their start and end apart: 9 -> 9, of which waited for: 5 -> 5; matrix products, arithmetic and copies ran while one was open for 0% -> 1% of each run, Pallas kernels for 0% -> 0%
where the time goes in v1:
time: 149 us; the launch traced here: 148 us
  blocking collectives  77.6 us (52%)
  waiting for transfers between devices  27.4 us (18%)
  starting transfers between devices  21.8 us (15%)
  other arithmetic  12.8 us (9%)
  local copies, waits for them, and re-layouts  7.37 us (5%)
    psum x2, blocking collectives, local(): lax.psum(lax.psum((sizes_local, weighted), 'gx'), ('gy', 'gz'))  62.5 us
    psum x2, blocking collectives, local(): lax.psum((sizes_local, weighted), 'gx')  15.1 us
    ppermute x4, waiting for transfers between devices, with_halo(): lax.ppermute(lax.slice_in_dim(block, block.shape[dim] - width, None, axis...  14.8 us
    ppermute x4, starting transfers between devices, with_halo(): lax.ppermute(lax.slice_in_dim(block, block.shape[dim] - width, None, axis...  13.2 us
    ppermute x4, waiting for transfers between devices, with_halo(): lax.ppermute(lax.slice_in_dim(block, 0, width, axis=dim), axis, backward)  12.6 us
    ppermute x4, starting transfers between devices, with_halo(): lax.ppermute(lax.slice_in_dim(block, 0, width, axis=dim), axis, backward)  5.16 us
    unnamed x36, local copies, waits for them, and re-layouts  4.52 us
    all_to_all x1, starting transfers between devices, local(): lax.all_to_all(labelling, 'gy', split_axis=2, concat_axis=1, tiled=True)  3.41 us
  transfers between devices with their start and end apart: 9, of which 5 were waited for; matrix products, arithmetic and copies ran while one was open for 1% of the time, Pallas kernels for 0%

profile of v1, /device:TPU:0, one launch (start us, length us, event | category | flops | bytes accessed | tf_op | source)
XLA Modules:
  0.0 147.9 jit_solution(249447750562619487)
XLA Ops:
  1.3 0.9 multiply_subtract_fusion.1
  3.0 1.0 subtract_maximum_fusion.2
  4.0 2.4 %collective-permute-start = (f32[4,1,64,128]{3,2,1,0:T(8,128)S(1)}, f32[4,1,64,128]{3,2,1,0:T(8,128)S(1)}, u32[]{:S(2)}, u32[]{:S(2)}) collective-permute-start(f32[4,1,64,128]{3,2,1,0:T(8,128)S(1)} %get-tuple-element.28), channel_id=1, source_target_pairs={{0,4},{4,8},{8,12},{12,16},{16,20},{20,24},{24,28},{1,5},{5,9},{9,... | collective-permute-start | bytes 393224 | tf_op jit(solution)/shard_map/ppermute | solution.py:18
  6.4 1.3 collective-permute-start.1
  8.0 3.7 %collective-permute-done.1 = f32[4,1,64,128]{3,2,1,0:T(8,128)S(1)} collective-permute-done((f32[4,1,64,128]{3,2,1,0:T(8,128)S(1)}, f32[4,1,64,128]{3,2,1,0:T(8,128)S(1)}, u32[]{:S(2)}, u32[]{:S(2)}) %collective-permute-start.1) | collective-permute-done | bytes 131104 | tf_op jit(solution)/shard_map/ppermute | solution.py:21
  12.0 3.5 %collective-permute-start.2 = (f32[4,4,64,1]{3,2,1,0:T(8,128)S(1)}, f32[4,4,64,1]{3,2,1,0:T(8,128)S(1)}, u32[]{:S(2)}, u32[]{:S(2)}) collective-permute-start(f32[4,4,64,1]{3,2,1,0:T(8,128)S(1)} %get-tuple-element.23), channel_id=1, source_target_pairs={{0,1},{1,2},{2,3},{4,5},{5,6},{6,7},{8,9},{9,10},{10,11},{12,13},{... | collective-permute-start | bytes 12296 | tf_op jit(solution)/shard_map/ppermute | solution.py:18
  15.5 1.3 collective-permute-start.3
  16.8 8.4 %collective-permute-done.2 = f32[4,4,64,1]{3,2,1,0:T(8,128)S(1)} collective-permute-done((f32[4,4,64,1]{3,2,1,0:T(8,128)S(1)}, f32[4,4,64,1]{3,2,1,0:T(8,128)S(1)}, u32[]{:S(2)}, u32[]{:S(2)}) %collective-permute-start.2) | collective-permute-done | bytes 4128 | tf_op jit(solution)/shard_map/ppermute | solution.py:18
  25.2 4.7 %collective-permute-done.3 = f32[4,4,64,1]{3,2,1,0:T(8,128)S(1)} collective-permute-done((f32[4,4,64,1]{3,2,1,0:T(8,128)S(1)}, f32[4,4,64,1]{3,2,1,0:T(8,128)S(1)}, u32[]{:S(2)}, u32[]{:S(2)}) %collective-permute-start.3) | collective-permute-done | bytes 4128 | tf_op jit(solution)/shard_map/ppermute | solution.py:21
  34.1 1.2 multiply_reduce_fusion.1
  36.7 4.7 %collective-permute-start.4 = (f32[4,1,64,128]{3,2,1,0:T(8,128)}, f32[4,1,64,128]{3,2,1,0:T(8,128)}, u32[]{:S(2)}, u32[]{:S(2)}) collective-permute-start(f32[4,1,64,128]{3,2,1,0:T(8,128)} %get-tuple-element.26), channel_id=1, source_target_pairs={{0,4},{4,8},{8,12},{12,16},{16,20},{20,24},{24,28},{1,5},{5,9},{9,... | collective-permute-start | bytes 393224 | tf_op jit(solution)/shard_map/ppermute | solution.py:18
  41.3 1.3 collective-permute-start.5
  42.6 10.2 %all-reduce.5 = (f32[4]{0:T(128)}, f32[4]{0:T(128)}) all-reduce(f32[4]{0:T(128)} %get-tuple-element.3, f32[4]{0:T(128)} %get-tuple-element.2), channel_id=1, replica_groups=mesh['gx'=2,'gy'=4,'gz'=4] {'gx'}, use_global_device_ids=true, to_apply=%region_4.5 | all-reduce | flops 8 | bytes 64 | tf_op jit(solution)/shard_map/psum | solution.py:93
  52.8 31.9 %all-reduce.3 = (f32[4]{0:T(128)}, f32[4]{0:T(128)}) all-reduce(f32[4]{0:T(128)} %get-tuple-element.12, f32[4]{0:T(128)} %get-tuple-element.13), channel_id=1, replica_groups=mesh['gx'=2,'gy'=4,'gz'=4] {'gy','gz'}, use_global_device_ids=true, to_apply=%region_5.6 | all-reduce | flops 8 | bytes 64 | tf_op jit(solution)/shard_map/psum | solution.py:93
  84.7 1.1 pad_maximum_fusion.2
  86.1 2.7 %collective-permute-start.6 = (f32[4,4,64,1]{3,2,1,0:T(8,128)S(1)}, f32[4,4,64,1]{3,2,1,0:T(8,128)S(1)}, u32[]{:S(2)}, u32[]{:S(2)}) collective-permute-start(f32[4,4,64,1]{3,2,1,0:T(8,128)S(1)} %get-tuple-element.21), channel_id=1, source_target_pairs={{0,1},{1,2},{2,3},{4,5},{5,6},{6,7},{8,9},{9,10},{10,11},{12,13},{... | collective-permute-start | bytes 12296 | tf_op jit(solution)/shard_map/ppermute | solution.py:18
  88.7 1.3 collective-permute-start.7
  90.1 6.4 %collective-permute-done.6 = f32[4,4,64,1]{3,2,1,0:T(8,128)S(1)} collective-permute-done((f32[4,4,64,1]{3,2,1,0:T(8,128)S(1)}, f32[4,4,64,1]{3,2,1,0:T(8,128)S(1)}, u32[]{:S(2)}, u32[]{:S(2)}) %collective-permute-start.6) | collective-permute-done | bytes 4128 | tf_op jit(solution)/shard_map/ppermute | solution.py:18
  96.4 4.1 %collective-permute-done.7 = f32[4,4,64,1]{3,2,1,0:T(8,128)S(1)} collective-permute-done((f32[4,4,64,1]{3,2,1,0:T(8,128)S(1)}, f32[4,4,64,1]{3,2,1,0:T(8,128)S(1)}, u32[]{:S(2)}, u32[]{:S(2)}) %collective-permute-start.7) | collective-permute-done | bytes 4128 | tf_op jit(solution)/shard_map/ppermute | solution.py:21
  100.6 1.5 %select_maximum_fusion = f32[4,4,66,130]{3,2,1,0:T(8,128)S(1)} fusion(f32[4,4,64,1]{3,2,1,0:T(8,128)S(1)} %collective-permute-done.7, f32[4,4,64,1]{3,2,1,0:T(8,128)S(1)} %collective-permute-done.6, f32[4,1,64,128]{3,2,1,0:T(8,128)} %collective-permute-done.5, f32[4,2,64,128]{3,2,1,0:T(8,128)S(1)} %copy-done.3, f32[4,1,64,128]{3,2,1,0:T(8,128)} %collective-permute-done.4), kind=kLoop, calls=%fused_computation.8 | loop fusion | flops 1647360 | bytes 1081600 | tf_op jit(solution)/shard_map/concatenate | solution.py:22
  104.5 1.2 copy-done.1
  107.7 3.4 %all-to-all-start = ((f32[4,2,64,128]{3,1,0,2:T(2,128)}), f32[4,2,64,128]{3,1,0,2:T(2,128)S(1)}, u32[]{:S(2)}, u32[]{:S(2)}) async-start(f32[4,2,64,128]{3,1,0,2:T(2,128)} %copy.8), calls=%async_computation | async-start | bytes 524288 | tf_op jit(solution)/shard_map/all_to_all | solution.py:95
  111.1 4.9 %all-reduce.4 = (f32[4]{0:T(128)S(1)}, f32[4]{0:T(128)S(1)}) all-reduce(f32[4]{0:T(128)S(1)} %get-tuple-element.5, f32[4]{0:T(128)S(1)} %get-tuple-element.4), channel_id=1, replica_groups=mesh['gx'=2,'gy'=4,'gz'=4] {'gx'}, use_global_device_ids=true, to_apply=%region_10.11 | all-reduce | flops 8 | bytes 64 | tf_op jit(solution)/shard_map/psum | solution.py:93
  116.0 30.6 %all-reduce.2 = (f32[4]{0:T(128)S(1)}, f32[4]{0:T(128)S(1)}) all-reduce(f32[4]{0:T(128)S(1)} %get-tuple-element.10, f32[4]{0:T(128)S(1)} %get-tuple-element.11), channel_id=1, replica_groups=mesh['gx'=2,'gy'=4,'gz'=4] {'gy','gz'}, use_global_device_ids=true, to_apply=%region_11.12 | all-reduce | flops 8 | bytes 64 | tf_op jit(solution)/shard_map/psum | solution.py:93
  (73 shorter events, 13.3 us)
Async XLA Ops:
  4.0 4.0 %collective-permute-start = (f32[4,1,64,128]{3,2,1,0:T(8,128)S(1)}, f32[4,1,64,128]{3,2,1,0:T(8,128)S(1)}, u32[]{:S(2)}, u32[]{:S(2)}) collective-permute-start(f32[4,1,64,128]{3,2,1,0:T(8,128)S(1)} %get-tuple-element.28), channel_id=1, source_target_pairs={{0,4},{4,8},{8,12},{12,16},{16,20},{20,24},{24,28},{1,5},{5,9},{9,... | collective-permute-start | bytes 393224 | tf_op jit(solution)/shard_map/ppermute | solution.py:18
  6.4 5.3 %collective-permute-start.1 = (f32[4,1,64,128]{3,2,1,0:T(8,128)S(1)}, f32[4,1,64,128]{3,2,1,0:T(8,128)S(1)}, u32[]{:S(2)}, u32[]{:S(2)}) collective-permute-start(f32[4,1,64,128]{3,2,1,0:T(8,128)S(1)} %get-tuple-element.29), channel_id=1, source_target_pairs={{4,0},{8,4},{12,8},{16,12},{20,16},{24,20},{28,24},{5,1},{9,5},{13... | collective-permute-start | bytes 393224 | tf_op jit(solution)/shard_map/ppermute | solution.py:21
  7.9 23.2 %copy-start.6 = (f32[3,65,129]{2,1,0:T(8,128)}, f32[3,65,129]{2,1,0:T(8,128)S(1)}, u32[]{:S(2)}) copy-start(f32[3,65,129]{2,1,0:T(8,128)S(1)} %and_convert_fusion) | copy-start | bytes 301864
  12.0 13.2 %collective-permute-start.2 = (f32[4,4,64,1]{3,2,1,0:T(8,128)S(1)}, f32[4,4,64,1]{3,2,1,0:T(8,128)S(1)}, u32[]{:S(2)}, u32[]{:S(2)}) collective-permute-start(f32[4,4,64,1]{3,2,1,0:T(8,128)S(1)} %get-tuple-element.23), channel_id=1, source_target_pairs={{0,1},{1,2},{2,3},{4,5},{5,6},{6,7},{8,9},{9,10},{10,11},{12,13},{... | collective-permute-start | bytes 12296 | tf_op jit(solution)/shard_map/ppermute | solution.py:18
  15.5 14.4 %collective-permute-start.3 = (f32[4,4,64,1]{3,2,1,0:T(8,128)S(1)}, f32[4,4,64,1]{3,2,1,0:T(8,128)S(1)}, u32[]{:S(2)}, u32[]{:S(2)}) collective-permute-start(f32[4,4,64,1]{3,2,1,0:T(8,128)S(1)} %get-tuple-element.24), channel_id=1, source_target_pairs={{1,0},{2,1},{3,2},{5,4},{6,5},{7,6},{9,8},{10,9},{11,10},{13,12},{... | collective-permute-start | bytes 12296 | tf_op jit(solution)/shard_map/ppermute | solution.py:21
  16.8 14.1 %copy-start.14 = (pred[65]{0:T(512)(128)(4,1)}, pred[65]{0:T(512)(128)(4,1)S(1)}, u32[]{:S(2)}) copy-start(pred[65]{0:T(512)(128)(4,1)S(1)} %fusion.62) | copy-start | bytes 199
  31.7 0.9 copy-start.9
  32.6 1.5 %copy-start = (f32[4,3,3,65,129]{4,3,2,0,1:T(8,128)}, f32[4,3,3,65,129]{4,3,2,0,1:T(8,128)S(1)}, u32[]{:S(2)}) copy-start(f32[4,3,3,65,129]{4,3,2,0,1:T(8,128)S(1)} %fusion.1) | copy-start | bytes 3622324
  34.1 2.6 %copy-start.11 = (f32[2,64,128]{2,1,0:T(8,128)}, f32[2,64,128]{2,1,0:T(8,128)S(1)}, u32[]{:S(2)}) copy-start(f32[2,64,128]{2,1,0:T(8,128)S(1)} %maximum_bitcast_fusion.1) | copy-start | bytes 196612
  34.1 55.9 %copy-start.13 = (s32[4]{0:T(128)S(1)}, s32[4]{0:T(128)}, u32[]{:S(2)}) copy-start(s32[4]{0:T(128)} %param.3) | copy-start | bytes 52
  36.7 48.0 %collective-permute-start.4 = (f32[4,1,64,128]{3,2,1,0:T(8,128)}, f32[4,1,64,128]{3,2,1,0:T(8,128)}, u32[]{:S(2)}, u32[]{:S(2)}) collective-permute-start(f32[4,1,64,128]{3,2,1,0:T(8,128)} %get-tuple-element.26), channel_id=1, source_target_pairs={{0,4},{4,8},{8,12},{12,16},{16,20},{20,24},{24,28},{1,5},{5,9},{9,... | collective-permute-start | bytes 393224 | tf_op jit(solution)/shard_map/ppermute | solution.py:18
  41.3 43.4 %collective-permute-start.5 = (f32[4,1,64,128]{3,2,1,0:T(8,128)}, f32[4,1,64,128]{3,2,1,0:T(8,128)}, u32[]{:S(2)}, u32[]{:S(2)}) collective-permute-start(f32[4,1,64,128]{3,2,1,0:T(8,128)} %get-tuple-element.27), channel_id=1, source_target_pairs={{4,0},{8,4},{12,8},{16,12},{20,16},{24,20},{28,24},{5,1},{9,5},{13... | collective-permute-start | bytes 393224 | tf_op jit(solution)/shard_map/ppermute | solution.py:21
  84.7 5.4 %copy-start.16 = (f32[4]{0:T(128)S(1)}, f32[4]{0:T(128)}, u32[]{:S(2)}) copy-start(f32[4]{0:T(128)} %get-tuple-element.8) | copy-start | bytes 52
  84.7 5.4 %copy-start.17 = (f32[4]{0:T(128)S(1)}, f32[4]{0:T(128)}, u32[]{:S(2)}) copy-start(f32[4]{0:T(128)} %get-tuple-element.9) | copy-start | bytes 52
  84.7 15.9 %copy-start.3 = (f32[4,2,64,128]{3,2,1,0:T(8,128)S(1)}, f32[4,2,64,128]{3,2,1,0:T(8,128)}, u32[]{:S(2)}) copy-start(f32[4,2,64,128]{3,2,1,0:T(8,128)} %copy-done.2) | copy-start | bytes 786436
  85.8 16.3 %copy-start.15 = (pred[65]{0:T(512)(128)(4,1)S(1)}, pred[65]{0:T(512)(128)(4,1)}, u32[]{:S(2)}) copy-start(pred[65]{0:T(512)(128)(4,1)} %copy-done.14) | copy-start | bytes 199
  86.1 10.4 %collective-permute-start.6 = (f32[4,4,64,1]{3,2,1,0:T(8,128)S(1)}, f32[4,4,64,1]{3,2,1,0:T(8,128)S(1)}, u32[]{:S(2)}, u32[]{:S(2)}) collective-permute-start(f32[4,4,64,1]{3,2,1,0:T(8,128)S(1)} %get-tuple-element.21), channel_id=1, source_target_pairs={{0,1},{1,2},{2,3},{4,5},{5,6},{6,7},{8,9},{9,10},{10,11},{12,13},{... | collective-permute-start | bytes 12296 | tf_op jit(solution)/shard_map/ppermute | solution.py:18
  88.7 11.9 %collective-permute-start.7 = (f32[4,4,64,1]{3,2,1,0:T(8,128)S(1)}, f32[4,4,64,1]{3,2,1,0:T(8,128)S(1)}, u32[]{:S(2)}, u32[]{:S(2)}) collective-permute-start(f32[4,4,64,1]{3,2,1,0:T(8,128)S(1)} %get-tuple-element.22), channel_id=1, source_target_pairs={{1,0},{2,1},{3,2},{5,4},{6,5},{7,6},{9,8},{10,9},{11,10},{13,12},{... | collective-permute-start | bytes 12296 | tf_op jit(solution)/shard_map/ppermute | solution.py:21
  102.5 0.9 copy-start.7
  104.0 1.8 %copy-start.1 = (f32[4,3,3,65,129]{4,3,2,0,1:T(8,128)S(1)}, f32[4,3,3,65,129]{4,3,2,0,1:T(8,128)}, u32[]{:S(2)}) copy-start(f32[4,3,3,65,129]{4,3,2,0,1:T(8,128)} %copy-done) | copy-start | bytes 3622324
  104.0 1.7 %copy-start.5 = (f32[2,64,128]{2,1,0:T(8,128)S(1)}, f32[2,64,128]{2,1,0:T(8,128)}, u32[]{:S(2)}) copy-start(f32[2,64,128]{2,1,0:T(8,128)} %param.2) | copy-start | bytes 196612
  104.0 1.7 %copy-start.10 = (f32[2,64,128]{2,1,0:T(8,128)S(1)}, f32[2,64,128]{2,1,0:T(8,128)}, u32[]{:S(2)}) copy-start(f32[2,64,128]{2,1,0:T(8,128)} %copy-done.8) | copy-start | bytes 196612
  104.0 1.7 %copy-start.12 = (f32[2,64,128]{2,1,0:T(8,128)S(1)}, f32[2,64,128]{2,1,0:T(8,128)}, u32[]{:S(2)}) copy-start(f32[2,64,128]{2,1,0:T(8,128)} %copy-done.11) | copy-start | bytes 196612
  107.7 39.5 %all-to-all-start = ((f32[4,2,64,128]{3,1,0,2:T(2,128)}), f32[4,2,64,128]{3,1,0,2:T(2,128)S(1)}, u32[]{:S(2)}, u32[]{:S(2)}) async-start(f32[4,2,64,128]{3,1,0,2:T(2,128)} %copy.8), calls=%async_computation | async-start | bytes 524288 | tf_op jit(solution)/shard_map/all_to_all | solution.py:95
  (3 other events, 2.2 us)
